TPU v7x, 32 devices: a whole 2x2x4 slice. The times are simulated.
32 devices in a mesh: dp: 8 (over y, x, core), mp: 4 (over z).
Axes of the slice: x: 2, y: 2, z: 4, core: 2. Of those that a mesh axis runs over, the one named last changes fastest.
Arguments:
- grad_parts: bfloat16 [8, 4, 1024, 4096], P('dp', None, None, 'mp'), may hold values from -4000 to 4000
- master: float32 [4, 1024, 4096], P(None, 'dp', 'mp'), may hold values from -6 to 6
- first_moment: float32 [4, 1024, 4096], P(None, 'dp', 'mp'), may hold values from -4 to 4
- second_moment: float32 [4, 1024, 4096], P(None, 'dp', 'mp'), may hold values from 0.25 to 4
- left_basis: bfloat16 [4, 1024, 4096], P(None, 'dp', 'mp'), may hold values from -1 to 1, as said below
- right_basis: bfloat16 [4, 1024, 4096], P(None, 'dp', 'mp'), may hold values from -1 to 1, as said below
Outputs:
- weights: bfloat16 [4, 1024, 4096], P(None, None, 'mp')
- new_master: float32 [4, 1024, 4096], P(None, 'dp', 'mp')
- new_first: float32 [4, 1024, 4096], P(None, 'dp', 'mp')
- new_second: float32 [4, 1024, 4096], P(None, 'dp', 'mp')
Inputs may be any that keep to these rules, and one draw needn't show every extreme that they name: Each block left_basis[i, :, j * 1024 : (j + 1) * 1024] is an orthogonal 1024 x 1024 matrix up to rounding. Each block right_basis[i, :, j * 1024 : (j + 1) * 1024] is an orthogonal 1024 x 1024 matrix up to rounding.
All inputs are finite; a program needn't handle non-finite values.
Results may differ from a plain program's by a relative error of at most 0.02.
Values may be sent and summed in bfloat16 or wider, within the bound.
A program may use at most 128 MiB of HBM per device.

v0:
```python
import jax
import jax.numpy as jnp
from jax import lax
from jax.sharding import PartitionSpec as P

D = 4096
STEP = 10
beta_one = 0.95
beta_two = 0.95
epsilon = 1e-08
norm_epsilon = 1e-06
learning_rate = 0.3
decay_rate = 0.1


def per_device(grad_parts, master, first_moment, second_moment, left_basis, right_basis):
    gradient = lax.psum_scatter(grad_parts[0], "dp", scatter_dimension=1, tiled=True).astype(
        jnp.float32
    )
    squares_sum = lax.psum(jnp.sum(gradient * gradient), ("dp", "mp"))
    clip_scale = jnp.minimum(1.0, 2.0 * D / jnp.sqrt(squares_sum + norm_epsilon))
    grad_low = gradient.astype(jnp.bfloat16)
    right_full = lax.all_gather(right_basis, "dp", axis=1, tiled=True)
    turned = jnp.einsum(
        "isk,ikb->isb", grad_low, right_full, preferred_element_type=jnp.float32
    ).astype(jnp.bfloat16)
    left_cols = left_basis
    raw_term = jnp.einsum("isx,isb->xib", left_cols, turned, preferred_element_type=jnp.float32)
    rotated_rows = lax.psum_scatter(
        lax.optimization_barrier(raw_term.astype(jnp.bfloat16))
        .astype(jnp.float32)
        .astype(jnp.bfloat16),
        "dp",
        scatter_dimension=0,
        tiled=True,
    ).astype(jnp.float32)
    rotated = jnp.transpose(rotated_rows, (1, 0, 2))
    clipped = clip_scale * rotated
    new_first = beta_one * first_moment + (1.0 - beta_one) * clipped
    new_second = beta_two * second_moment + (1.0 - beta_two) * clipped * clipped
    bias_one = 1.0 - beta_one**STEP
    bias_two = 1.0 - beta_two**STEP
    direction = (new_first / bias_one / (jnp.sqrt(new_second / bias_two) + epsilon)).astype(
        jnp.bfloat16
    )
    back_rows = jnp.einsum(
        "isb,icb->isc", direction, right_full, preferred_element_type=jnp.float32
    ).astype(jnp.bfloat16)
    left_cols = left_basis
    update = jnp.einsum(
        "isk,ikc->isc",
        left_cols,
        lax.all_gather(back_rows, "dp", axis=1, tiled=True),
        preferred_element_type=jnp.float32,
    )
    new_master = master * (1.0 - learning_rate * decay_rate) - learning_rate * update
    weights = lax.all_gather(new_master.astype(jnp.bfloat16), "dp", axis=1, tiled=True)
    return (weights, new_master, new_first, new_second)


def solution(mesh):
    return jax.shard_map(
        per_device,
        mesh=mesh,
        in_specs=(
            P("dp", None, None, "mp"),
            P(None, "dp", "mp"),
            P(None, "dp", "mp"),
            P(None, "dp", "mp"),
            P(None, "dp", "mp"),
            P(None, "dp", "mp"),
        ),
        out_specs=(
            P(None, None, "mp"),
            P(None, "dp", "mp"),
            P(None, "dp", "mp"),
            P(None, "dp", "mp"),
        ),
        check_vma=False,
    )
```

profile of v0, /device:TPU:0, one launch (start us, length us, event | category | flops | bytes accessed | tf_op | source)
XLA Modules:
  0.0 386.3 jit_solution(4198887484840549487)
XLA Ops:
  7.2 0.0 reduce-scatter.5.cloned.1.call-start
  7.2 0.7 reduce-scatter.5.cloned.1.call-update
  7.9 0.0 all-gather.4.cloned.1.call-start
  8.0 0.7 all-gather.4.cloned.1.call-update
  8.7 0.0 reduce-scatter.7.cloned.1.call-start
  8.7 77.0 %reduce-scatter.5.cloned.1.call-done = bf16[4,128,1024]{2,1,0:T(8,128)(2,1)} async-done(((bf16[4,1024,1024]{2,1,0:T(8,128)(2,1)}), bf16[4,128,1024]{2,1,0:T(8,128)(2,1)}) %reduce-scatter.5.cloned.1.call-update) | async-done | bytes 1048592 | tf_op jit(solution)/shard_map/reduce_scatter | solution.py:17
  85.7 56.2 %all-gather.4.cloned.1.call-done = bf16[4,1024,1024]{2,1,0:T(8,128)(2,1)} async-done(((bf16[4,128,1024]{2,1,0:T(8,128)(2,1)}), bf16[4,1024,1024]{2,1,0:T(8,128)(2,1)}) %all-gather.4.cloned.1.call-update) | async-done | bytes 8388624 | tf_op jit(solution)/shard_map/all_gather | solution.py:23
  141.9 9.2 %convert_bitcast_fusion = bf16[1024,4,1024]{0,2,1:T(8,128)(2,1)} fusion(bf16[4,128,1024]{2,1,0:T(8,128)(2,1)S(1)} %copy-done, bf16[4,128,1024]{2,1,0:T(8,128)(2,1)} %reduce-scatter.5.cloned.1.call-done, bf16[4,1024,1024]{2,1,0:T(8,128)(2,1)} %all-gather.4.cloned.1.call-done), kind=kOutput, calls=%fused_computation | convolution fusion | flops 2152202240 | bytes 18874368 | tf_op jit(solution)/shard_map/isx,isb->xib/dot_general | solution.py:28
  151.1 11.8 %copy.26 = bf16[1024,4096]{1,0:T(8,128)(2,1)} copy(bf16[1024,4096]{0,1:T(8,128)(2,1)} %bitcast.17) | data formatting | bytes 16777216
  162.9 0.0 reduce-scatter.7.cloned.1.call-update
  162.9 0.0 all-gather.6.cloned.1.call-start
  162.9 1.9 copy.18
  164.8 2.4 multiply_reduce_fusion
  167.2 3.3 copy.19
  170.5 39.7 %psum.7 = f32[]{:T(128)} all-reduce(f32[]{:T(128)} %multiply_reduce_fusion), channel_id=1, replica_groups=mesh['dp'=8,'mp'=4] {'dp','mp'}, use_global_device_ids=true, to_apply=%region_2.0 | all-reduce | flops 1 | bytes 8 | tf_op jit(solution)/shard_map/psum | solution.py:20
  210.9 24.3 %reduce-scatter.7.cloned.1.call-done = bf16[128,4096]{1,0:T(8,128)(2,1)} async-done(((bf16[1024,4096]{1,0:T(8,128)(2,1)}), bf16[128,4096]{1,0:T(8,128)(2,1)}) %reduce-scatter.7.cloned.1.call-update) | async-done | bytes 1048592
  235.2 2.3 copy.27
  237.5 2.5 multiply_add_fusion
  240.0 1.3 copy-done.1
  241.3 0.7 copy-done.2
  242.0 7.0 %convolution_convert_fusion = bf16[4,128,1024]{1,2,0:T(8,128)(2,1)} fusion(bf16[4,1024,1024]{2,1,0:T(8,128)(2,1)} %all-gather.4.cloned.1.call-done, f32[4,128,1024]{1,2,0:T(8,128)S(1)} %get-tuple-element.13, f32[4,128,1024]{1,2,0:T(8,128)S(1)} %get-tuple-element.12), kind=kOutput, calls=%fused_computation.8 | convolution fusion | flops 1076887552 | bytes 13631488 | tf_op jit(solution)/shard_map/isb,icb->isc/dot_general | solution.py:46
  249.0 0.0 all-gather.6.cloned.1.call-update
  249.0 0.0 all-gather.8.cloned.1.call-start
  249.0 1.8 copy.17
  250.9 54.1 %all-gather.6.cloned.1.call-done = bf16[4,1024,1024]{1,2,0:T(8,128)(2,1)} async-done(((bf16[4,128,1024]{1,2,0:T(8,128)(2,1)}), bf16[4,1024,1024]{1,2,0:T(8,128)(2,1)}) %all-gather.6.cloned.1.call-update) | async-done | bytes 8388624 | tf_op jit(solution)/shard_map/all_gather | solution.py:53
  305.0 7.4 %fusion.5 = (bf16[4,128,1024]{1,2,0:T(8,128)(2,1)}, f32[4,128,1024]{1,2,0:T(8,128)S(1)}) fusion(bf16[4,1024,1024]{1,2,0:T(8,128)(2,1)} %all-gather.6.cloned.1.call-done, bf16[4,128,1024]{2,1,0:T(8,128)(2,1)S(1)} %copy-done, f32[4,128,1024]{1,2,0:T(8,128)} %copy.17), kind=kOutput, calls=%fused_computation.14 | convolution fusion | flops 1075838976 | bytes 14680064 | tf_op jit(solution)/shard_map/isk,ikc->isc/dot_general | solution.py:50
  312.4 0.0 all-gather.8.cloned.1.call-update
  312.4 2.9 copy.22
  315.3 2.9 copy.23
  318.2 1.8 copy.21
  320.0 48.4 %all-gather.8.cloned.1.call-done = bf16[4,1024,1024]{1,2,0:T(8,128)(2,1)} async-done(((bf16[4,128,1024]{1,2,0:T(8,128)(2,1)}), bf16[4,1024,1024]{1,2,0:T(8,128)(2,1)}) %all-gather.8.cloned.1.call-update) | async-done | bytes 8388624 | tf_op jit(solution)/shard_map/all_gather | solution.py:57
  368.4 11.3 %copy.20 = bf16[4,1024,1024]{2,1,0:T(8,128)(2,1)} copy(bf16[4,1024,1024]{1,2,0:T(8,128)(2,1)} %all-gather.8.cloned.1.call-done) | data formatting | bytes 16777216
  (6 shorter events, 0.0 us)
Async XLA Ops:
  7.2 134.7 %copy-start = (bf16[4,128,1024]{2,1,0:T(8,128)(2,1)S(1)}, bf16[4,128,1024]{2,1,0:T(8,128)(2,1)}, u32[]{:S(2)}) copy-start(bf16[4,128,1024]{2,1,0:T(8,128)(2,1)} %param.10) | copy-start | bytes 3145732
  7.2 78.5 %reduce-scatter.5.cloned.1.call-start = ((), (), s32[]{:S(2)}) async-start(), calls=%async_computation.2 | async-start | bytes 9437184 | tf_op jit(solution)/shard_map/reduce_scatter | solution.py:17
  7.9 134.0 %all-gather.4.cloned.1.call-start = ((), (), s32[]{:S(2)}) async-start(), calls=%async_computation.3 | async-start | bytes 9437184 | tf_op jit(solution)/shard_map/all_gather | solution.py:23
  8.7 226.6 %reduce-scatter.7.cloned.1.call-start = ((), (), s32[]{:S(2)}) async-start(), calls=%async_computation.6 | async-start | bytes 9437184
  162.9 142.1 %all-gather.6.cloned.1.call-start = ((), (), s32[]{:S(2)}) async-start(), calls=%async_computation.4 | async-start | bytes 9437184 | tf_op jit(solution)/shard_map/all_gather | solution.py:53
  239.9 1.3 copy-start.1
  240.0 2.0 copy-start.2
  242.0 7.1 %copy-start.3 = (f32[4,128,1024]{2,1,0:T(8,128)S(1)}, f32[4,128,1024]{2,1,0:T(8,128)}, u32[]{:S(2)}) copy-start(f32[4,128,1024]{2,1,0:T(8,128)} %param.7) | copy-start | bytes 6291460
  249.0 119.5 %all-gather.8.cloned.1.call-start = ((), (), s32[]{:S(2)}) async-start(), calls=%async_computation.5 | async-start | bytes 9437184 | tf_op jit(solution)/shard_map/all_gather | solution.py:57
Sparse Core Ops, SparseCore 0:
  11.4 74.2 reduce-scatter.4
  87.6 54.2 all-gather.3
  163.0 72.1 reduce-scatter.6
  249.1 55.8 all-gather.5
  312.5 55.8 all-gather.7
where the time goes:
time: 387 us; the launch traced here: 386 us
  waiting for transfers between devices  262 us (68%)
  local copies, waits for them, and re-layouts  41.9 us (11%)
  blocking collectives  39.7 us (10%)
  matrix products  23.6 us (6%)
  between operations  14.5 us (4%)
  other arithmetic  4.83 us (1%)
    reduce_scatter x1, waiting for transfers between devices, per_device(): lax.psum_scatter(grad_parts[0], 'dp', scatter_dimension=1, tiled=True)  77 us
    all_gather x1, waiting for transfers between devices, per_device(): right_full = lax.all_gather(right_basis, 'dp', axis=1, tiled=True)  56.2 us
    all_gather x1, waiting for transfers between devices, per_device(): lax.all_gather(back_rows, 'dp', axis=1, tiled=True)  54.1 us
    all_gather x1, waiting for transfers between devices, per_device(): lax.all_gather(new_master.astype(jnp.bfloat16), 'dp', axis=1, tiled=True)  48.4 us
    unnamed x17, local copies, waits for them, and re-layouts  41.9 us
    psum x1, blocking collectives, per_device(): squares_sum = lax.psum(jnp.sum(gradient * gradient), ('dp', 'mp'))  39.7 us
    unnamed x6, waiting for transfers between devices  25.7 us
    dot_general x1, matrix products, per_device(): jnp.einsum('isx,isb->xib', left_cols, turned, preferred_element_type=jnp....  9.19 us
  transfers between devices with their start and end apart: 5, of which 5 were waited for; matrix products, arithmetic and copies ran while one was open for 4% of the time, Pallas kernels for 0%

commit v1 on v0

--- a/solution.py
+++ b/solution.py
@@ -11,6 +11,22 @@
 norm_epsilon = 1e-06
 learning_rate = 0.3
 decay_rate = 0.1
+
+
+def product_in_turn(x, axis, dim, contribution):
+    devices, here, rows = (lax.axis_size(axis), lax.axis_index(axis), x.shape[dim])
+    ahead = [(i, (i + 1) % devices) for i in range(devices)]
+    backward = [(i, (i - 1) % devices) for i in range(devices)]
+    middle = devices // 2
+    from_left = from_right = x
+    subtotal = contribution(x, here * rows)
+    for step in range(1, middle + 1):
+        from_left = lax.ppermute(from_left, axis, ahead)
+        if step < devices - middle:
+            from_right = lax.ppermute(from_right, axis, backward)
+            subtotal = subtotal + contribution(from_right, (here + step) % devices * rows)
+        subtotal = subtotal + contribution(from_left, (here - step) % devices * rows)
+    return subtotal
 
 
 def per_device(grad_parts, master, first_moment, second_moment, left_basis, right_basis):
@@ -47,11 +63,16 @@
         "isb,icb->isc", direction, right_full, preferred_element_type=jnp.float32
     ).astype(jnp.bfloat16)
     left_cols = left_basis
-    update = jnp.einsum(
-        "isk,ikc->isc",
-        left_cols,
-        lax.all_gather(back_rows, "dp", axis=1, tiled=True),
-        preferred_element_type=jnp.float32,
+    update = product_in_turn(
+        back_rows,
+        "dp",
+        1,
+        lambda own_block, offset: jnp.einsum(
+            "isk,ikc->isc",
+            lax.dynamic_slice_in_dim(left_cols, offset, own_block.shape[1], axis=2),
+            own_block,
+            preferred_element_type=jnp.float32,
+        ),
     )
     new_master = master * (1.0 - learning_rate * decay_rate) - learning_rate * update
     weights = lax.all_gather(new_master.astype(jnp.bfloat16), "dp", axis=1, tiled=True)

time: 387 us -> 413 us (1.067)
  waiting for transfers between devices: 262 us -> 285 us
  local copies, waits for them, and re-layouts: 41.9 us -> 33.9 us
  starting transfers between devices: 0.2 us -> 6.34 us
  matrix products: 23.6 us -> 28.6 us
    ppermute x0 -> x7, waiting for transfers between devices: none -> 76.1 us  [the longest x4 76.1 us: product_in_turn(): from_left = lax.ppermute(from_left, axis, ahead)]
    all_gather x1 -> x0, waiting for transfers between devices: 54.1 us -> none  [per_device(): lax.all_gather(back_rows, 'dp', axis=1, tiled=True)]
    unnamed x17 -> x21, local copies, waits for them, and re-layouts: 41.9 us -> 33.9 us
    ppermute x0 -> x7, starting transfers between devices: none -> 6.18 us  [the longest x3 6.12 us: product_in_turn(): from_right = lax.ppermute(from_right, axis, backward)]
    dot_general x1 -> x8, matrix products: 7.4 us -> 11.9 us  [per_device(): jnp.einsum('isk,ikc->isc', lax.dynamic_slice_in_dim(left_cols, offset, ow...]
    unnamed x6 -> x5, waiting for transfers between devices: 25.7 us -> 26 us
  transfers between devices with their start and end apart: 5 -> 11, of which waited for: 5 -> 8; matrix products, arithmetic and copies ran while one was open for 4% -> 5% of each run, Pallas kernels for 0% -> 0%
where the time goes in v1:
time: 413 us; the launch traced here: 412 us
  waiting for transfers between devices  285 us (69%)
  blocking collectives  39.9 us (10%)
  local copies, waits for them, and re-layouts  33.9 us (8%)
  matrix products  28.6 us (7%)
  between operations  14.6 us (4%)
  starting transfers between devices  6.34 us (2%)
  other arithmetic  4.22 us (1%)
    reduce_scatter x1, waiting for transfers between devices, per_device(): lax.psum_scatter(grad_parts[0], 'dp', scatter_dimension=1, tiled=True)  77 us
    ppermute x4, waiting for transfers between devices, product_in_turn(): from_left = lax.ppermute(from_left, axis, ahead)  76.1 us
    all_gather x1, waiting for transfers between devices, per_device(): right_full = lax.all_gather(right_basis, 'dp', axis=1, tiled=True)  56.2 us
    all_gather x1, waiting for transfers between devices, per_device(): lax.all_gather(new_master.astype(jnp.bfloat16), 'dp', axis=1, tiled=True)  49.5 us
    psum x1, blocking collectives, per_device(): squares_sum = lax.psum(jnp.sum(gradient * gradient), ('dp', 'mp'))  39.9 us
    unnamed x21, local copies, waits for them, and re-layouts  33.9 us
    unnamed x5, waiting for transfers between devices  26 us
    dot_general x8, matrix products, per_device(): jnp.einsum('isk,ikc->isc', lax.dynamic_slice_in_dim(left_cols, offset, ow...  11.9 us
  transfers between devices with their start and end apart: 11, of which 8 were waited for; matrix products, arithmetic and copies ran while one was open for 5% of the time, Pallas kernels for 0%

profile of v1, /device:TPU:0, one launch (start us, length us, event | category | flops | bytes accessed | tf_op | source)
XLA Modules:
  0.0 412.3 jit_solution(14110599128187330156)
XLA Ops:
  8.0 0.7 all-gather.3.cloned.1.call-update
  8.7 77.0 %reduce-scatter.5.cloned.1.call-done = bf16[4,128,1024]{2,1,0:T(8,128)(2,1)} async-done(((bf16[4,1024,1024]{2,1,0:T(8,128)(2,1)}), bf16[4,128,1024]{2,1,0:T(8,128)(2,1)}) %reduce-scatter.5.cloned.1.call-update) | async-done | bytes 1048592 | tf_op jit(solution)/shard_map/reduce_scatter | solution.py:33
  85.7 56.2 %all-gather.3.cloned.1.call-done = bf16[4,1024,1024]{2,1,0:T(8,128)(2,1)} async-done(((bf16[4,128,1024]{2,1,0:T(8,128)(2,1)}), bf16[4,1024,1024]{2,1,0:T(8,128)(2,1)}) %all-gather.3.cloned.1.call-update) | async-done | bytes 8388624 | tf_op jit(solution)/shard_map/all_gather | solution.py:39
  141.9 9.2 %convert_bitcast_fusion = bf16[1024,4,1024]{0,2,1:T(8,128)(2,1)} fusion(bf16[4,128,1024]{2,1,0:T(8,128)(2,1)S(1)} %copy-done, bf16[4,128,1024]{2,1,0:T(8,128)(2,1)} %reduce-scatter.5.cloned.1.call-done, bf16[4,1024,1024]{2,1,0:T(8,128)(2,1)} %all-gather.3.cloned.1.call-done), kind=kOutput, calls=%fused_computation | convolution fusion | flops 2152202240 | bytes 18874368 | tf_op jit(solution)/shard_map/isx,isb->xib/dot_general | solution.py:44
  151.1 11.3 %copy.23 = bf16[1024,4096]{1,0:T(8,128)(2,1)} copy(bf16[1024,4096]{0,1:T(8,128)(2,1)} %bitcast.21) | data formatting | bytes 16777216
  162.5 3.0 copy.15
  165.4 1.1 multiply_reduce_fusion
  166.6 3.1 copy.16
  169.6 39.9 %psum.7 = f32[]{:T(128)} all-reduce(f32[]{:T(128)} %multiply_reduce_fusion), channel_id=1, replica_groups=mesh['dp'=8,'mp'=4] {'dp','mp'}, use_global_device_ids=true, to_apply=%region_2.0 | all-reduce | flops 1 | bytes 8 | tf_op jit(solution)/shard_map/psum | solution.py:36
  210.2 24.6 %reduce-scatter.7.cloned.1.call-done = bf16[128,4096]{1,0:T(8,128)(2,1)} async-done(((bf16[1024,4096]{1,0:T(8,128)(2,1)}), bf16[128,4096]{1,0:T(8,128)(2,1)}) %reduce-scatter.7.cloned.1.call-update) | async-done | bytes 1048592
  234.8 2.3 copy.24
  237.0 3.1 multiply_add_fusion
  240.1 7.5 %convolution_convert_fusion = bf16[4,128,1024]{2,1,0:T(8,128)(2,1)S(1)} fusion(bf16[4,1024,1024]{2,1,0:T(8,128)(2,1)} %all-gather.3.cloned.1.call-done, f32[4,128,1024]{1,2,0:T(8,128)S(1)} %get-tuple-element.13, f32[4,128,1024]{1,2,0:T(8,128)S(1)} %get-tuple-element.12), kind=kOutput, calls=%fused_computation.8 | convolution fusion | flops 1076887552 | bytes 13631488 | tf_op jit(solution)/shard_map/isb,icb->isc/dot_general | solution.py:62
  247.7 0.9 copy-done.4
  248.6 1.7 collective-permute-start
  250.3 22.8 %collective-permute-done.1 = bf16[4,128,1024]{2,1,0:T(8,128)(2,1)S(1)} collective-permute-done((bf16[4,128,1024]{2,1,0:T(8,128)(2,1)S(1)}, bf16[4,128,1024]{2,1,0:T(8,128)(2,1)S(1)}, u32[]{:S(2)}, u32[]{:S(2)}) %collective-permute-start.1) | collective-permute-done | bytes 1048608 | tf_op jit(solution)/shard_map/ppermute | solution.py:24
  273.1 1.0 copy-done.5
  274.1 1.7 collective-permute-start.2
  275.8 23.3 %collective-permute-done.3 = bf16[4,128,1024]{2,1,0:T(8,128)(2,1)} collective-permute-done((bf16[4,128,1024]{2,1,0:T(8,128)(2,1)S(1)}, bf16[4,128,1024]{2,1,0:T(8,128)(2,1)}, u32[]{:S(2)}, u32[]{:S(2)}) %collective-permute-start.3) | collective-permute-done | bytes 1048608 | tf_op jit(solution)/shard_map/ppermute | solution.py:24
  299.1 1.7 fusion.16
  301.3 2.7 collective-permute-start.4
  304.0 1.6 fusion.14
  305.7 20.0 %collective-permute-done.5 = bf16[4,128,1024]{2,1,0:T(8,128)(2,1)} collective-permute-done((bf16[4,128,1024]{2,1,0:T(8,128)(2,1)}, bf16[4,128,1024]{2,1,0:T(8,128)(2,1)}, u32[]{:S(2)}, u32[]{:S(2)}) %collective-permute-start.5) | collective-permute-done | bytes 1048608 | tf_op jit(solution)/shard_map/ppermute | solution.py:24
  325.7 1.6 fusion.8
  327.3 1.7 fusion.10
  329.0 1.7 fusion.4
  331.1 9.9 %collective-permute-done.6 = bf16[4,128,1024]{2,1,0:T(8,128)(2,1)S(1)} collective-permute-done((bf16[4,128,1024]{2,1,0:T(8,128)(2,1)}, bf16[4,128,1024]{2,1,0:T(8,128)(2,1)S(1)}, u32[]{:S(2)}, u32[]{:S(2)}) %collective-permute-start.6) | collective-permute-done | bytes 1048608 | tf_op jit(solution)/shard_map/ppermute | solution.py:24
  341.0 2.8 fusion.28
  343.8 2.9 copy.18
  346.7 1.8 copy.19
  348.5 49.5 %all-gather.5.cloned.1.call-done = bf16[4,1024,1024]{2,1,0:T(8,128)(2,1)} async-done(((bf16[4,128,1024]{2,1,0:T(8,128)(2,1)}), bf16[4,1024,1024]{2,1,0:T(8,128)(2,1)}) %all-gather.5.cloned.1.call-update) | async-done | bytes 8388624 | tf_op jit(solution)/shard_map/all_gather | solution.py:78
  398.0 7.8 %copy.26 = bf16[4,1024,1024]{2,1,0:T(8,128)(2,1)} copy(bf16[4,1024,1024]{2,1,0:T(8,128)(2,1)} %all-gather.5.cloned.1.call-done) | data formatting | bytes 16777216
  (28 shorter events, 1.8 us)
Async XLA Ops:
  7.2 134.7 %copy-start = (bf16[4,128,1024]{2,1,0:T(8,128)(2,1)S(1)}, bf16[4,128,1024]{2,1,0:T(8,128)(2,1)}, u32[]{:S(2)}) copy-start(bf16[4,128,1024]{2,1,0:T(8,128)(2,1)} %param.10) | copy-start | bytes 3145732
  7.2 78.5 %reduce-scatter.5.cloned.1.call-start = ((), (), s32[]{:S(2)}) async-start(), calls=%async_computation.2 | async-start | bytes 9437184 | tf_op jit(solution)/shard_map/reduce_scatter | solution.py:33
  7.9 134.0 %all-gather.3.cloned.1.call-start = ((), (), s32[]{:S(2)}) async-start(), calls=%async_computation.3 | async-start | bytes 9437184 | tf_op jit(solution)/shard_map/all_gather | solution.py:39
  8.7 226.1 %reduce-scatter.7.cloned.1.call-start = ((), (), s32[]{:S(2)}) async-start(), calls=%async_computation.5 | async-start | bytes 9437184
  162.4 3.0 copy-start.2
  162.4 235.6 %all-gather.5.cloned.1.call-start = ((), (), s32[]{:S(2)}) async-start(), calls=%async_computation.4 | async-start | bytes 9437184 | tf_op jit(solution)/shard_map/all_gather | solution.py:78
  240.1 7.5 %copy-start.1 = (f32[4,128,1024]{1,2,0:T(8,128)}, f32[4,128,1024]{1,2,0:T(8,128)S(1)}, u32[]{:S(2)}) copy-start(f32[4,128,1024]{1,2,0:T(8,128)S(1)} %get-tuple-element.12) | copy-start | bytes 6291460
  247.6 1.0 copy-start.4
  247.6 25.5 %collective-permute-start.1 = (bf16[4,128,1024]{2,1,0:T(8,128)(2,1)S(1)}, bf16[4,128,1024]{2,1,0:T(8,128)(2,1)S(1)}, u32[]{:S(2)}, u32[]{:S(2)}) collective-permute-start(bf16[4,128,1024]{2,1,0:T(8,128)(2,1)S(1)} %convolution_convert_fusion), channel_id=1, source_target_pairs={{0,4},{4,8},{8,12},{12,16},{16,20},{20,24},{24,28},{28,0},{1,5},{5... | collective-permute-start | bytes 3145736 | tf_op jit(solution)/shard_map/ppermute | solution.py:24
  248.6 24.6 %collective-permute-start = (bf16[4,128,1024]{2,1,0:T(8,128)(2,1)S(1)}, bf16[4,128,1024]{2,1,0:T(8,128)(2,1)}, u32[]{:S(2)}, u32[]{:S(2)}) collective-permute-start(bf16[4,128,1024]{2,1,0:T(8,128)(2,1)S(1)} %convolution_convert_fusion), channel_id=1, source_target_pairs={{0,28},{4,0},{8,4},{12,8},{16,12},{20,16},{24,20},{28,24},{1,29},{... | collective-permute-start | bytes 3145736 | tf_op jit(solution)/shard_map/ppermute | solution.py:26
  273.1 1.0 copy-start.5
  273.1 26.0 %collective-permute-start.3 = (bf16[4,128,1024]{2,1,0:T(8,128)(2,1)S(1)}, bf16[4,128,1024]{2,1,0:T(8,128)(2,1)}, u32[]{:S(2)}, u32[]{:S(2)}) collective-permute-start(bf16[4,128,1024]{2,1,0:T(8,128)(2,1)S(1)} %collective-permute-done.1), channel_id=1, source_target_pairs={{0,4},{4,8},{8,12},{12,16},{16,20},{20,24},{24,28},{28,0},{1,5},{5... | collective-permute-start | bytes 3145736 | tf_op jit(solution)/shard_map/ppermute | solution.py:24
  274.1 27.2 %collective-permute-start.2 = (bf16[4,128,1024]{2,1,0:T(8,128)(2,1)}, bf16[4,128,1024]{2,1,0:T(8,128)(2,1)}, u32[]{:S(2)}, u32[]{:S(2)}) collective-permute-start(bf16[4,128,1024]{2,1,0:T(8,128)(2,1)} %collective-permute-done), channel_id=1, source_target_pairs={{0,28},{4,0},{8,4},{12,8},{16,12},{20,16},{24,20},{28,24},{1,29},{... | collective-permute-start | bytes 3145736 | tf_op jit(solution)/shard_map/ppermute | solution.py:26
  299.1 26.5 %collective-permute-start.5 = (bf16[4,128,1024]{2,1,0:T(8,128)(2,1)}, bf16[4,128,1024]{2,1,0:T(8,128)(2,1)}, u32[]{:S(2)}, u32[]{:S(2)}) collective-permute-start(bf16[4,128,1024]{2,1,0:T(8,128)(2,1)} %collective-permute-done.3), channel_id=1, source_target_pairs={{0,4},{4,8},{8,12},{12,16},{16,20},{20,24},{24,28},{28,0},{1,5},{5... | collective-permute-start | bytes 3145736 | tf_op jit(solution)/shard_map/ppermute | solution.py:24
  299.1 1.7 copy-start.6
  301.3 29.3 %collective-permute-start.4 = (bf16[4,128,1024]{2,1,0:T(8,128)(2,1)}, bf16[4,128,1024]{2,1,0:T(8,128)(2,1)S(1)}, u32[]{:S(2)}, u32[]{:S(2)}) collective-permute-start(bf16[4,128,1024]{2,1,0:T(8,128)(2,1)} %collective-permute-done.2), channel_id=1, source_target_pairs={{0,28},{4,0},{8,4},{12,8},{16,12},{20,16},{24,20},{28,24},{1,29},{... | collective-permute-start | bytes 3145736 | tf_op jit(solution)/shard_map/ppermute | solution.py:26
  325.7 15.3 %collective-permute-start.6 = (bf16[4,128,1024]{2,1,0:T(8,128)(2,1)}, bf16[4,128,1024]{2,1,0:T(8,128)(2,1)S(1)}, u32[]{:S(2)}, u32[]{:S(2)}) collective-permute-start(bf16[4,128,1024]{2,1,0:T(8,128)(2,1)} %collective-permute-done.5), channel_id=1, source_target_pairs={{0,4},{4,8},{8,12},{12,16},{16,20},{20,24},{24,28},{28,0},{1,5},{5... | collective-permute-start | bytes 3145736 | tf_op jit(solution)/shard_map/ppermute | solution.py:24
  330.6 10.4 %copy-start.3 = (f32[4,128,1024]{2,1,0:T(8,128)S(1)}, f32[4,128,1024]{2,1,0:T(8,128)}, u32[]{:S(2)}) copy-start(f32[4,128,1024]{2,1,0:T(8,128)} %param.7) | copy-start | bytes 6291460
Sparse Core Ops, SparseCore 0:
  11.4 74.2 reduce-scatter.4
  87.6 54.2 all-gather.2
  162.5 72.1 reduce-scatter.6
  343.9 54.0 all-gather.4
